TPU v7x, 512 devices: a whole 4x8x8 slice. The times are simulated.
512 devices in a mesh: ctx: 256 (over z, y, x_hi, core), tp: 2 (over x_lo).
Axes of the slice: x: 4 (x_hi: 2, x_lo: 2; x = x_hi * 2 + x_lo), y: 8, z: 8, core: 2. Of those that a mesh axis runs over, the one named last changes fastest.
Arguments:
- queries: bfloat16 [16384, 16, 128], P('ctx', 'tp'), may hold values from -6 to 6
- incoming_lookup_vectors: bfloat16 [16384, 4, 128], P('ctx', 'tp'), may hold values from -6 to 6
- incoming_content_vectors: bfloat16 [16384, 4, 128], P('ctx', 'tp'), may hold values from -6 to 6
Outputs:
- attention: bfloat16 [16384, 16, 128], P(('ctx', 'tp'))
- key_cache: bfloat16 [16384, 4, 128], P('ctx', 'tp')
All inputs are finite; a program needn't handle non-finite values.
Results may differ from a plain program's by a relative error of at most 0.0075.
Values may be sent and summed in bfloat16 or wider, within the bound.
A program may use at most 128 MiB of HBM per device.

v0:
```python
import functools
import math

import jax
import jax.numpy as jnp
import numpy as np
from jax import lax
from jax.experimental import pallas as pl
from jax.experimental.pallas import tpu as pltpu
from jax.sharding import PartitionSpec as P

rope_base = 500000.0
MESH = pl.DeviceIdType.MESH
ROW = 4
RING = 8
ORDER = (0, 1, 7, 2, 6, 3, 5, 4)
MAJOR = -1
FAR, NEAR = 4, 3
NEVER = -1e30


def angle_tables(blocks, rows, width):
    half = width // 2
    freq = rope_base ** (-(np.arange(half, dtype=np.float64) * 2.0 / width))
    freq = np.concatenate([freq, freq])[None, :]
    fine = np.arange(rows, dtype=np.float64)[:, None] * freq
    coarse = np.arange(blocks, dtype=np.float64)[:, None] * rows * freq
    fine_table = np.stack([np.cos(fine), np.sin(fine)]).astype(np.float32)
    coarse_table = np.stack([np.cos(coarse), np.sin(coarse)], 1).astype(np.float32)
    coarse_table = np.broadcast_to(coarse_table[:, :, None, :], (blocks, 2, 8, width))
    return fine_table, np.ascontiguousarray(coarse_table)


def kernel(
    heads,
    kv_heads,
    q_hbm,
    k_hbm,
    v_hbm,
    fine_hbm,
    coarse_hbm,
    att_hbm,
    cache_hbm,
    q_in,
    k_in,
    v_in,
    fine,
    coarse,
    wide_kv,
    wide_q,
    kv_own,
    kv,
    q_send,
    q_all,
    run_max,
    run_acc,
    out_send,
    out_recv,
    stat_send,
    stat_recv,
    wide_out,
    att_vmem,
    cache_vmem,
    load_sem,
    store_sem,
    twin_send,
    twin_recv,
    first_send,
    first_recv,
    unit_send,
    unit_recv,
    q_send_sem,
    q_recv_sem,
    out_send_sem,
    out_recv_sem,
    stat_send_sem,
    stat_recv_sem,
):
    rows = k_in.shape[0] // kv_heads
    width = k_in.shape[1]
    half_width = width // 2
    group = heads // kv_heads
    keep = rows // 2
    span = 2 * rows
    piece = group * keep
    keys = RING * span
    me = lax.axis_index("ctx")
    part = lax.axis_index("tp")
    core = me % 2
    x_hi = (me // 2) % 2
    y_at = (me // ROW) % RING
    z_at = me // (ROW * RING)
    along_y = 1 - core
    a = along_y * y_at + core * z_at
    u = along_y * z_at + core * y_at
    first_stride = along_y * ROW + core * ROW * RING
    second_stride = along_y * ROW * RING + core * ROW
    row_base = me - me % ROW
    twin = me + 1 - 2 * core
    place = (me % ROW) * 2 + part

    def first_peer(f):
        return me + (f - a) * first_stride

    def second_peer(w):
        return me + (w - u) * second_stride

    def up_by(value, d):
        return lax.rem(value + d + RING, RING)

    def row_peer(d):
        return {"ctx": row_base + d // 2, "tp": d % 2}

    loads = [
        pltpu.make_async_copy(k_hbm, k_in, load_sem.at[0]),
        pltpu.make_async_copy(v_hbm, v_in, load_sem.at[1]),
        pltpu.make_async_copy(fine_hbm, fine, load_sem.at[2]),
        pltpu.make_async_copy(coarse_hbm.at[me], coarse, load_sem.at[3]),
        pltpu.make_async_copy(q_hbm, q_in, load_sem.at[4]),
    ]
    barrier = pltpu.get_barrier_semaphore()
    for d in range(1, RING):
        to = first_peer(up_by(a, d))
        pl.semaphore_signal(barrier, inc=1, device_id={"ctx": to}, device_id_type=MESH)
    for d in (1, -1):
        to = second_peer(up_by(u, d))
        pl.semaphore_signal(barrier, inc=1, device_id={"ctx": to}, device_id_type=MESH)
    for i in range(1, 8):
        to = row_peer(lax.rem(place + i, 8))
        pl.semaphore_signal(barrier, inc=1, device_id=to, device_id_type=MESH)

    for load in loads:
        load.start()

    loads[2].wait()
    loads[3].wait()
    cos_c = coarse[0, 0:1, :]
    sin_c = coarse[1, 0:1, :]
    cosine = cos_c * fine[0] - sin_c * fine[1]
    sine = sin_c * fine[0] + cos_c * fine[1]
    lane = lax.broadcasted_iota(jnp.int32, (rows, width), 1)
    sine = jnp.where(lane < half_width, -sine, sine)

    def turn(x):
        return x * cosine + pltpu.roll(x, half_width, 1) * sine

    loads[0].wait()
    loads[1].wait()
    wide_kv[0] = k_in[...].astype(jnp.float32)
    wide_kv[1] = v_in[...].astype(jnp.float32)
    for j in range(kv_heads):
        take = pl.ds(j, rows, stride=kv_heads)
        key_rot = turn(wide_kv[0, take, :])
        wide_kv[0, take, :] = key_rot
        kv_own[j, 0] = key_rot.astype(jnp.bfloat16)
        kv_own[j, 1] = wide_kv[1, take, :].astype(jnp.bfloat16)
    kv[u, a, core] = kv_own[core]
    cache_vmem[...] = wide_kv[0].astype(jnp.bfloat16)
    cache_store = pltpu.make_async_copy(cache_vmem, cache_hbm, store_sem.at[0])
    cache_store.start()

    pl.semaphore_wait(barrier, (RING - 1) + 2 + 7)

    def twin_copy(unit, f, half):
        return pltpu.make_async_remote_copy(
            src_ref=kv_own.at[1 - core],
            dst_ref=kv.at[unit, f, half],
            send_sem=twin_send,
            recv_sem=twin_recv,
            device_id={"ctx": twin},
            device_id_type=MESH,
        )

    twin_copy(a, u, core).start()

    loads[4].wait()
    wide_q[...] = q_in[...].astype(jnp.float32)
    for h in range(heads):
        turned = turn(wide_q[pl.ds(h, rows, stride=heads), :]).astype(jnp.bfloat16)
        for half in range(2):
            q_send[h // group, half, h % group] = turned[half * keep : (half + 1) * keep]

    def first_copy(f, to, slot):
        return pltpu.make_async_remote_copy(
            src_ref=kv.at[u, f],
            dst_ref=kv.at[u, f],
            send_sem=first_send.at[slot],
            recv_sem=first_recv.at[f],
            device_id={"ctx": to},
            device_id_type=MESH,
        )

    def unit_copy(unit, f, to, slot):
        return pltpu.make_async_remote_copy(
            src_ref=kv.at[unit, f],
            dst_ref=kv.at[unit, f],
            send_sem=unit_send.at[slot, f],
            recv_sem=unit_recv.at[unit, f],
            device_id={"ctx": to},
            device_id_type=MESH,
        )

    major_to = second_peer(up_by(u, MAJOR))
    minor_to = second_peer(up_by(u, -MAJOR))

    twin_copy(u, a, 1 - core).wait_recv()
    for i in range(1, RING):
        first_copy(a, first_peer(up_by(a, ORDER[i])), i).start()
    unit_copy(u, a, major_to, 0).start()
    unit_copy(u, a, minor_to, 1).start()

    own_slot = me % ROW

    def q_copy(slot, to_slot, index):
        return pltpu.make_async_remote_copy(
            src_ref=q_send.at[to_slot % 2],
            dst_ref=q_all.at[slot],
            send_sem=q_send_sem.at[index],
            recv_sem=q_recv_sem.at[slot],
            device_id={"ctx": row_base + to_slot},
            device_id_type=MESH,
        )

    for i in range(1, ROW):
        q_copy(own_slot, lax.rem(own_slot + i, ROW), i).start()
    q_all[own_slot] = q_send[core]
    run_max[...] = jnp.full(run_max.shape, NEVER, jnp.float32)
    run_acc[...] = jnp.zeros(run_acc.shape, jnp.float32)

    for i in range(1, RING):
        f = up_by(a, ORDER[i])
        first_copy(f, me, i).wait_recv()
        unit_copy(u, f, major_to, 0).start()
        unit_copy(u, f, minor_to, 1).start()
    for i in range(1, ROW):
        slot = lax.rem(own_slot + i, ROW)
        q_copy(slot, own_slot, i).wait_recv()

    factor = math.log2(math.e) / math.sqrt(width)
    unit_step = along_y * (span * 2 * RING) + core * span * 2
    block_step = along_y * span * 2 + core * (span * 2 * RING)
    row_start = (z_at * RING + y_at) * span * 2

    def absorb(unit):
        key_block = kv[unit, :, :, 0].reshape(keys, width)
        value_block = kv[unit, :, :, 1].reshape(keys, width)
        extended = jnp.concatenate([value_block, jnp.ones_like(value_block)], axis=1)

        def chunk(r, carry):
            q = q_all[r].reshape(2 * piece, width)
            scores = factor * lax.dot_general(
                q, key_block, (((1,), (1,)), ((), ())), preferred_element_type=jnp.float32
            )
            at = lax.broadcasted_iota(jnp.int32, (2 * piece, 1), 0)
            q_at = row_start + (2 * r + at // piece) * keep + at % keep
            col = lax.broadcasted_iota(jnp.int32, (1, keys), 1)
            k_at = unit * unit_step + (col // span) * block_step + x_hi * span + col % span
            scores = jnp.where(k_at <= q_at, scores, NEVER)
            take = pl.ds(pl.multiple_of(r * 2 * piece, 2 * piece), 2 * piece)
            old = run_max[take, 0:1]
            top = jnp.maximum(old, jnp.max(scores, axis=1, keepdims=True))
            weights = jnp.exp2(scores - top).astype(jnp.bfloat16)
            total = jnp.dot(weights, extended, preferred_element_type=jnp.float32)
            run_acc[take, :] = total + jnp.exp2(old - top) * run_acc[take, :]
            run_max[take, :] = jnp.broadcast_to(top, (2 * piece, width))
            return carry

        lax.fori_loop(0, ROW, chunk, 0)

    def step_of(step):
        d = (step + 1) // 2
        odd = step % 2
        unit = up_by(u, (1 - 2 * odd) * MAJOR * d)
        far = up_by(u, (2 * odd - 1) * MAJOR)
        return d, odd, unit, far

    def advance(step, carry):
        d, odd, unit, far = step_of(step)
        to = second_peer(far)

        @pl.when(step > 0)
        def _():
            for i in range(RING):
                f = up_by(a, ORDER[i])
                unit_copy(unit, f, me, 0).wait_recv()

                @pl.when(d < NEAR + odd * (FAR - NEAR))
                def _():
                    unit_copy(unit, f, to, step + 1).start()

        @pl.when((unit <= u) | ((core == 1) & (z_at > 0)))
        def _():
            absorb(unit)

        return carry

    lax.fori_loop(0, RING, advance, 0)

    def out_copy(slot, d, index):
        return pltpu.make_async_remote_copy(
            src_ref=out_send.at[d],
            dst_ref=out_recv.at[slot],
            send_sem=out_send_sem.at[index],
            recv_sem=out_recv_sem.at[slot],
            device_id=row_peer(d),
            device_id_type=MESH,
        )

    def stat_copy(slot, d, index):
        return pltpu.make_async_remote_copy(
            src_ref=stat_send.at[d],
            dst_ref=stat_recv.at[slot],
            send_sem=stat_send_sem.at[index],
            recv_sem=stat_recv_sem.at[slot],
            device_id=row_peer(d),
            device_id_type=MESH,
        )

    def finish(d):
        take = pl.ds(pl.multiple_of(d * piece, piece), piece)
        weight = run_acc[take, width:]
        stat = run_max[take, :] + math.log2(math.e) * jnp.log(weight)
        return (run_acc[take, :width] / weight).astype(jnp.bfloat16), stat.T[0:8]

    out_order = (4, 5, 6, 7, 2, 3, 1)
    for i in out_order:
        d = lax.rem(place + i, 8)
        out_send[d], stat_send[d] = finish(d)
        out_copy(place, d, i).start()
        stat_copy(place, d, i).start()
    out_recv[place], stat_recv[place] = finish(place)

    for i in out_order:
        slot = lax.rem(place + i, 8)
        out_copy(slot, place, i).wait_recv()
        stat_copy(slot, place, i).wait_recv()

    for core_from in range(2):
        for tp_from in range(2):
            low = core_from * 2 + tp_from
            wide_stat = [
                jnp.broadcast_to(stat_recv[s, 0:1, :], (piece, width)).T for s in (low, low + 4)
            ]
            gap = wide_stat[1] - wide_stat[0]
            merged = out_recv[low].astype(jnp.float32) / (1.0 + jnp.exp2(gap))
            merged = merged + out_recv[low + 4].astype(jnp.float32) / (1.0 + jnp.exp2(-gap))
            for g in range(group):
                head = tp_from * heads + core_from * group + g
                wide_out[pl.ds(head, keep, stride=2 * heads), :] = merged[g * keep : (g + 1) * keep]
    att_vmem[...] = wide_out[...].astype(jnp.bfloat16)
    att_store = pltpu.make_async_copy(att_vmem, att_hbm, store_sem.at[1])
    att_store.start()

    twin_copy(a, u, core).wait_send()
    for i in range(1, RING):
        first_copy(a, me, i).wait_send()
    for i in range(1, ROW):
        q_copy(own_slot, lax.rem(own_slot + i, ROW), i).wait_send()
    for i in out_order:
        out_copy(place, lax.rem(place + i, 8), i).wait_send()
        stat_copy(place, lax.rem(place + i, 8), i).wait_send()

    def drain(slot, carry):
        for f in range(RING):
            unit_copy(u, f, me, slot).wait_send()
        return carry

    lax.fori_loop(0, RING - 1, drain, 0)
    cache_store.wait()
    att_store.wait()


def build(ctx_size, queries, keys_in, values_in):
    rows, heads, width = queries.shape
    kv_heads = keys_in.shape[1]
    group = heads // kv_heads
    keep = rows // 2
    piece = group * keep
    fine, coarse = angle_tables(ctx_size, rows, width)
    f32, bf16 = jnp.float32, jnp.bfloat16

    hbm = pl.BlockSpec(memory_space=pl.ANY)
    dma = pltpu.SemaphoreType.DMA
    att, cache = pl.pallas_call(
        functools.partial(kernel, heads, kv_heads),
        out_shape=(
            jax.ShapeDtypeStruct((2 * heads * keep, width), bf16),
            jax.ShapeDtypeStruct((rows * kv_heads, width), bf16),
        ),
        in_specs=[hbm] * 5,
        out_specs=(hbm, hbm),
        scratch_shapes=[
            pltpu.VMEM((rows * heads, width), bf16),
            pltpu.VMEM((rows * kv_heads, width), bf16),
            pltpu.VMEM((rows * kv_heads, width), bf16),
            pltpu.VMEM((2, rows, width), f32),
            pltpu.VMEM((2, 8, width), f32),
            pltpu.VMEM((2, rows * kv_heads, width), f32),
            pltpu.VMEM((rows * heads, width), f32),
            pltpu.VMEM((kv_heads, 2, rows, width), bf16),
            pltpu.VMEM((RING, RING, 2, 2, rows, width), bf16),
            pltpu.VMEM((2, 2, group, keep, width), bf16),
            pltpu.VMEM((ROW, 2, group, keep, width), bf16),
            pltpu.VMEM((8 * piece, width), f32),
            pltpu.VMEM((8 * piece, 2 * width), f32),
            pltpu.VMEM((8, piece, width), bf16),
            pltpu.VMEM((8, piece, width), bf16),
            pltpu.VMEM((8, 8, piece), f32),
            pltpu.VMEM((8, 8, piece), f32),
            pltpu.VMEM((2 * heads * keep, width), f32),
            pltpu.VMEM((2 * heads * keep, width), bf16),
            pltpu.VMEM((rows * kv_heads, width), bf16),
            dma((5,)),
            dma((2,)),
            dma,
            dma,
            dma((RING,)),
            dma((RING,)),
            dma((RING - 1, RING)),
            dma((RING, RING)),
            dma((ROW,)),
            dma((ROW,)),
            dma((8,)),
            dma((8,)),
            dma((8,)),
            dma((8,)),
        ],
        compiler_params=pltpu.CompilerParams(collective_id=0, has_side_effects=True),
    )(
        queries.reshape(rows * heads, width),
        keys_in.reshape(rows * kv_heads, width),
        values_in.reshape(rows * kv_heads, width),
        jnp.asarray(fine),
        jnp.asarray(coarse),
    )
    return att.reshape(keep, 2 * heads, width), cache.reshape(rows, kv_heads, width)


def solution(mesh):
    ctx_size = mesh.shape["ctx"]

    def per_device(queries, incoming_lookup_vectors, incoming_content_vectors):
        return build(ctx_size, queries, incoming_lookup_vectors, incoming_content_vectors)

    return jax.shard_map(
        per_device,
        mesh=mesh,
        in_specs=(P("ctx", "tp", None), P("ctx", "tp", None), P("ctx", "tp", None)),
        out_specs=(P(("ctx", "tp"), None, None), P("ctx", "tp", None)),
        check_vma=False,
    )
```

profile of v0, /device:TPU:56, one launch (start us, length us, event | category | flops | bytes accessed | tf_op | source)
XLA Modules:
  0.0 68.7 jit_solution(3493234789094530438)
XLA Ops:
  0.6 65.1 %shard_map.68 = (bf16[512,128]{1,0:T(8,128)(2,1)}, bf16[128,128]{1,0:T(8,128)(2,1)}) custom-call(bf16[512,128]{1,0:T(8,128)(2,1)} %bitcast.5, bf16[128,128]{1,0:T(8,128)(2,1)} %bitcast.7, bf16[128,128]{1,0:T(8,128)(2,1)} %bitcast.8, f32[2,64,128]{2,1,0:T(8,128)} %constant.4.clone.fine_hbm, f32[256,2,8,128]{3,2,1,0:T(8,128)} %constant.5.clone.coarse_hbm), custom_call_target="tpu_custom_call" | custom-call | tf_op jit(solution)/shard_map/pallas_call | solution.py:384
  65.8 1.6 %copy.9 = bf16[32,16,128]{2,1,0:T(8,128)(2,1)} copy(bf16[32,16,128]{2,1,0:T(8,128)(2,1)} %bitcast.6) | data formatting | bytes 262144
  67.3 1.4 %copy.10 = bf16[64,2,128]{2,1,0:T(2,128)(2,1)} copy(bf16[64,2,128]{2,1,0:T(2,128)(2,1)} %bitcast.9) | data formatting | bytes 65536
where the time goes:
time: 68.9 us; the launch traced here: 68.7 us
  Pallas kernels  65.1 us (94%)
  local copies, waits for them, and re-layouts  2.96 us (4%)
    pallas_call x1, Pallas kernels, build(): pl.pallas_call(functools.partial(kernel, heads, kv_heads), out_shape=(jax...  65.1 us
    unnamed x2, local copies, waits for them, and re-layouts  2.96 us

commit v1 on v0

--- a/solution.py
+++ b/solution.py
@@ -17,6 +17,7 @@
 MAJOR = -1
 FAR, NEAR = 4, 3
 NEVER = -1e30
+CH, NB = 256, 2
 
 
 def angle_tables(blocks, rows, width):
@@ -54,6 +55,7 @@
     q_all,
     run_max,
     run_acc,
+    score_buf,
     out_send,
     out_recv,
     stat_send,
@@ -245,27 +247,33 @@
         key_block = kv[unit, :, :, 0].reshape(keys, width)
         value_block = kv[unit, :, :, 1].reshape(keys, width)
         extended = jnp.concatenate([value_block, jnp.ones_like(value_block)], axis=1)
-
-        def chunk(r, carry):
-            q = q_all[r].reshape(2 * piece, width)
+        col = lax.broadcasted_iota(jnp.int32, (1, keys), 1)
+        k_at = unit * unit_step + (col // span) * block_step + x_hi * span + col % span - row_start
+        at = lax.broadcasted_iota(jnp.int32, (CH, 1), 0)
+
+        def score(r):
+            q = q_all[...].reshape(8 * piece, width)[r * CH : (r + 1) * CH]
             scores = factor * lax.dot_general(
                 q, key_block, (((1,), (1,)), ((), ())), preferred_element_type=jnp.float32
             )
-            at = lax.broadcasted_iota(jnp.int32, (2 * piece, 1), 0)
-            q_at = row_start + (2 * r + at // piece) * keep + at % keep
-            col = lax.broadcasted_iota(jnp.int32, (1, keys), 1)
-            k_at = unit * unit_step + (col // span) * block_step + x_hi * span + col % span
-            scores = jnp.where(k_at <= q_at, scores, NEVER)
-            take = pl.ds(pl.multiple_of(r * 2 * piece, 2 * piece), 2 * piece)
+            q_at = ((r * CH + at) // piece) * keep + at % keep
+            score_buf[r % NB] = jnp.where(k_at <= q_at, scores, NEVER)
+
+        def weigh(r):
+            take = slice(r * CH, (r + 1) * CH)
             old = run_max[take, 0:1]
-            top = jnp.maximum(old, jnp.max(scores, axis=1, keepdims=True))
-            weights = jnp.exp2(scores - top).astype(jnp.bfloat16)
+            top = jnp.maximum(old, jnp.max(score_buf[r % NB], axis=1, keepdims=True))
+            weights = jnp.exp2(score_buf[r % NB] - top).astype(jnp.bfloat16)
             total = jnp.dot(weights, extended, preferred_element_type=jnp.float32)
             run_acc[take, :] = total + jnp.exp2(old - top) * run_acc[take, :]
-            run_max[take, :] = jnp.broadcast_to(top, (2 * piece, width))
-            return carry
-
-        lax.fori_loop(0, ROW, chunk, 0)
+            run_max[take, :] = jnp.broadcast_to(top, (CH, width))
+
+        chunks = 8 * piece // CH
+        score(0)
+        for r in range(chunks):
+            if r + 1 < chunks:
+                score(r + 1)
+            weigh(r)
 
     def step_of(step):
         d = (step + 1) // 2
@@ -403,6 +411,7 @@
             pltpu.VMEM((ROW, 2, group, keep, width), bf16),
             pltpu.VMEM((8 * piece, width), f32),
             pltpu.VMEM((8 * piece, 2 * width), f32),
+            pltpu.VMEM((NB, CH, RING * 2 * rows), f32),
             pltpu.VMEM((8, piece, width), bf16),
             pltpu.VMEM((8, piece, width), bf16),
             pltpu.VMEM((8, 8, piece), f32),

time: 68.9 us -> 60 us (0.87)
  the two profiles are of different devices: /device:TPU:56 before, /device:TPU:1 now
where the time goes in v1:
time: 60 us; the launch traced here: 59.7 us
  Pallas kernels  56.1 us (94%)
  local copies, waits for them, and re-layouts  2.96 us (5%)
  between operations  0.64 us (1%)
    pallas_call x1, Pallas kernels, build(): pl.pallas_call(functools.partial(kernel, heads, kv_heads), out_shape=(jax...  56.1 us
    unnamed x2, local copies, waits for them, and re-layouts  2.96 us

profile of v1, /device:TPU:1, one launch (start us, length us, event | category | flops | bytes accessed | tf_op | source)
XLA Modules:
  0.0 59.7 jit_solution(441939099936414474)
XLA Ops:
  0.6 56.1 %shard_map.68 = (bf16[512,128]{1,0:T(8,128)(2,1)}, bf16[128,128]{1,0:T(8,128)(2,1)}) custom-call(bf16[512,128]{1,0:T(8,128)(2,1)} %bitcast.5, bf16[128,128]{1,0:T(8,128)(2,1)} %bitcast.7, bf16[128,128]{1,0:T(8,128)(2,1)} %bitcast.8, f32[2,64,128]{2,1,0:T(8,128)} %constant.4.clone.fine_hbm, f32[256,2,8,128]{3,2,1,0:T(8,128)} %constant.5.clone.coarse_hbm), custom_call_target="tpu_custom_call" | custom-call | tf_op jit(solution)/shard_map/pallas_call | solution.py:392
  56.8 1.6 %copy.9 = bf16[32,16,128]{2,1,0:T(8,128)(2,1)} copy(bf16[32,16,128]{2,1,0:T(8,128)(2,1)} %bitcast.6) | data formatting | bytes 262144
  58.3 1.4 %copy.10 = bf16[64,2,128]{2,1,0:T(2,128)(2,1)} copy(bf16[64,2,128]{2,1,0:T(2,128)(2,1)} %bitcast.9) | data formatting | bytes 65536

commit v2 on v1

--- a/solution.py
+++ b/solution.py
@@ -40,7 +40,8 @@
     v_hbm,
     fine_hbm,
     coarse_hbm,
-    att_hbm,
+    out_recv,
+    stat_recv,
     cache_hbm,
     q_in,
     k_in,
@@ -57,11 +58,7 @@
     run_acc,
     score_buf,
     out_send,
-    out_recv,
     stat_send,
-    stat_recv,
-    wide_out,
-    att_vmem,
     cache_vmem,
     load_sem,
     store_sem,
@@ -160,7 +157,6 @@
     cache_vmem[...] = wide_kv[0].astype(jnp.bfloat16)
     cache_store = pltpu.make_async_copy(cache_vmem, cache_hbm, store_sem.at[0])
     cache_store.start()
-
     pl.semaphore_wait(barrier, (RING - 1) + 2 + 7)
 
     def twin_copy(unit, f, half):
@@ -173,21 +169,12 @@
             device_id_type=MESH,
         )
 
-    twin_copy(a, u, core).start()
-
-    loads[4].wait()
-    wide_q[...] = q_in[...].astype(jnp.float32)
-    for h in range(heads):
-        turned = turn(wide_q[pl.ds(h, rows, stride=heads), :]).astype(jnp.bfloat16)
-        for half in range(2):
-            q_send[h // group, half, h % group] = turned[half * keep : (half + 1) * keep]
-
-    def first_copy(f, to, slot):
+    def first_copy(f, half, to, slot):
         return pltpu.make_async_remote_copy(
-            src_ref=kv.at[u, f],
-            dst_ref=kv.at[u, f],
-            send_sem=first_send.at[slot],
-            recv_sem=first_recv.at[f],
+            src_ref=kv.at[u, f, half],
+            dst_ref=kv.at[u, f, half],
+            send_sem=first_send.at[slot, half],
+            recv_sem=first_recv.at[f, half],
             device_id={"ctx": to},
             device_id_type=MESH,
         )
@@ -202,17 +189,6 @@
             device_id_type=MESH,
         )
 
-    major_to = second_peer(up_by(u, MAJOR))
-    minor_to = second_peer(up_by(u, -MAJOR))
-
-    twin_copy(u, a, 1 - core).wait_recv()
-    for i in range(1, RING):
-        first_copy(a, first_peer(up_by(a, ORDER[i])), i).start()
-    unit_copy(u, a, major_to, 0).start()
-    unit_copy(u, a, minor_to, 1).start()
-
-    own_slot = me % ROW
-
     def q_copy(slot, to_slot, index):
         return pltpu.make_async_remote_copy(
             src_ref=q_send.at[to_slot % 2],
@@ -223,20 +199,82 @@
             device_id_type=MESH,
         )
 
+    def climbs(unit):
+        return (core == 1) | ((unit <= u) & (u < RING - 1))
+
+    def wraps(unit):
+        return (core == 1) | (unit < FAR)
+
+    def spread(half, i_list):
+        for i in i_list:
+            to = up_by(a, ORDER[i])
+
+            @pl.when((core == 0) | (to > a))
+            def _():
+                first_copy(a, half, first_peer(to), i).start()
+
+
+    major_to = second_peer(up_by(u, MAJOR))
+    minor_to = second_peer(up_by(u, -MAJOR))
+
+    twin_copy(a, u, core).start()
+    spread(core, (1, 2, 3, 4, 5, 6, 7))
+
+    own_slot = me % ROW
+    loads[4].wait()
+    wide_q[...] = q_in[...].astype(jnp.float32)
+    for h in range(heads):
+        turned = turn(wide_q[pl.ds(h, rows, stride=heads), :]).astype(jnp.bfloat16)
+        for half in range(2):
+            q_send[h // group, half, h % group] = turned[half * keep : (half + 1) * keep]
+
+    twin_copy(u, a, 1 - core).wait_recv()
+    spread(1 - core, (1, 2, 3, 4, 5, 6, 7))
+    pl.when(wraps(u))(lambda: unit_copy(u, a, major_to, 0).start())
+    pl.when(climbs(u))(lambda: unit_copy(u, a, minor_to, 1).start())
     for i in range(1, ROW):
         q_copy(own_slot, lax.rem(own_slot + i, ROW), i).start()
     q_all[own_slot] = q_send[core]
+    @pl.when(core == 1)
+    def _():
+        def clear(f, carry):
+            kv[:, f] = jnp.zeros((RING, 2, 2, rows, width), jnp.bfloat16)
+            return carry
+
+        lax.fori_loop(a + 1, RING, clear, 0)
+
     run_max[...] = jnp.full(run_max.shape, NEVER, jnp.float32)
     run_acc[...] = jnp.zeros(run_acc.shape, jnp.float32)
 
+    def next_hop(i):
+        return first_peer(up_by(a, 1 if ORDER[i] > RING // 2 else -1))
+
+    def pass_on(f, half, i, slot):
+        first_copy(f, half, next_hop(i), slot).start()
+        first_sends.append((half, slot))
+
+    def early(i):
+        f = up_by(a, ORDER[i])
+        for k, to in ((0, major_to), (1, minor_to)):
+            unit = up_by(u, (2 * k - 1) * MAJOR)
+            unit_copy(unit, f, me, 0).wait_recv()
+            unit_copy(unit, f, to, 2 + k).start()
+
     for i in range(1, RING):
         f = up_by(a, ORDER[i])
-        first_copy(f, me, i).wait_recv()
-        unit_copy(u, f, major_to, 0).start()
-        unit_copy(u, f, minor_to, 1).start()
-    for i in range(1, ROW):
-        slot = lax.rem(own_slot + i, ROW)
-        q_copy(slot, own_slot, i).wait_recv()
+
+        @pl.when((core == 0) | (f < a))
+        def _():
+            for half in range(2):
+                first_copy(f, half, me, i).wait_recv()
+
+            @pl.when(wraps(u))
+            def _():
+                unit_copy(u, f, major_to, 0).start()
+
+            @pl.when(climbs(u))
+            def _():
+                unit_copy(u, f, minor_to, 1).start()
 
     factor = math.log2(math.e) / math.sqrt(width)
     unit_step = along_y * (span * 2 * RING) + core * span * 2
@@ -288,13 +326,26 @@
 
         @pl.when(step > 0)
         def _():
+            lands = (core == 1) | jnp.where(odd == 1, unit < FAR, unit < u)
+            goes = (core == 1) | jnp.where(odd == 1, unit < FAR, (unit < u) & (u < RING - 1))
+            goes = goes & (d < NEAR + odd * (FAR - NEAR))
+
             for i in range(RING):
                 f = up_by(a, ORDER[i])
-                unit_copy(unit, f, me, 0).wait_recv()
-
-                @pl.when(d < NEAR + odd * (FAR - NEAR))
+
+                @pl.when(lands & ((core == 0) | (f <= a)))
                 def _():
-                    unit_copy(unit, f, to, step + 1).start()
+                    unit_copy(unit, f, me, 0).wait_recv()
+
+                    @pl.when(goes)
+                    def _():
+                        unit_copy(unit, f, to, step + 1).start()
+
+        @pl.when(step == 0)
+        def _():
+            for i in range(1, ROW):
+                slot = lax.rem(own_slot + i, ROW)
+                q_copy(slot, own_slot, i).wait_recv()
 
         @pl.when((unit <= u) | ((core == 1) & (z_at > 0)))
         def _():
@@ -336,13 +387,59 @@
         out_send[d], stat_send[d] = finish(d)
         out_copy(place, d, i).start()
         stat_copy(place, d, i).start()
-    out_recv[place], stat_recv[place] = finish(place)
+    out_send[place], stat_send[place] = finish(place)
+    keeps = [
+        pltpu.make_async_copy(out_send.at[place], out_recv.at[place], store_sem.at[1]),
+        pltpu.make_async_copy(stat_send.at[place], stat_recv.at[place], store_sem.at[2]),
+    ]
+    for copy in keeps:
+        copy.start()
 
     for i in out_order:
         slot = lax.rem(place + i, 8)
         out_copy(slot, place, i).wait_recv()
         stat_copy(slot, place, i).wait_recv()
 
+    twin_copy(a, u, core).wait_send()
+    for i in range(1, RING):
+
+        @pl.when((core == 0) | (up_by(a, ORDER[i]) > a))
+        def _():
+            for half in range(2):
+                first_copy(a, half, me, i).wait_send()
+
+    for i in range(1, ROW):
+        q_copy(own_slot, lax.rem(own_slot + i, ROW), i).wait_send()
+    for i in out_order:
+        out_copy(place, lax.rem(place + i, 8), i).wait_send()
+        stat_copy(place, lax.rem(place + i, 8), i).wait_send()
+
+    def drain(slot, carry):
+        d = slot // 2
+        odd = 1 - slot % 2
+        unit = up_by(u, (1 - 2 * odd) * MAJOR * d)
+        goes = (core == 1) | jnp.where(odd == 1, unit < FAR, (unit <= u) & (u < RING - 1))
+
+        @pl.when(goes)
+        def _():
+            for f in range(RING):
+
+                @pl.when((core == 0) | (f <= a))
+                def _():
+                    unit_copy(u, f, me, slot).wait_send()
+
+        return carry
+
+    lax.fori_loop(0, RING - 1, drain, 0)
+    cache_store.wait()
+    for copy in keeps:
+        copy.wait()
+
+
+def merge_kernel(heads, group, out_recv, stat_recv, cache_in, att, cache, wide_out):
+    _, piece, width = out_recv.shape
+    keep = piece // group
+    cache[...] = cache_in[...]
     for core_from in range(2):
         for tp_from in range(2):
             low = core_from * 2 + tp_from
@@ -355,27 +452,7 @@
             for g in range(group):
                 head = tp_from * heads + core_from * group + g
                 wide_out[pl.ds(head, keep, stride=2 * heads), :] = merged[g * keep : (g + 1) * keep]
-    att_vmem[...] = wide_out[...].astype(jnp.bfloat16)
-    att_store = pltpu.make_async_copy(att_vmem, att_hbm, store_sem.at[1])
-    att_store.start()
-
-    twin_copy(a, u, core).wait_send()
-    for i in range(1, RING):
-        first_copy(a, me, i).wait_send()
-    for i in range(1, ROW):
-        q_copy(own_slot, lax.rem(own_slot + i, ROW), i).wait_send()
-    for i in out_order:
-        out_copy(place, lax.rem(place + i, 8), i).wait_send()
-        stat_copy(place, lax.rem(place + i, 8), i).wait_send()
-
-    def drain(slot, carry):
-        for f in range(RING):
-            unit_copy(u, f, me, slot).wait_send()
-        return carry
-
-    lax.fori_loop(0, RING - 1, drain, 0)
-    cache_store.wait()
-    att_store.wait()
+    att[...] = wide_out[...].astype(jnp.bfloat16)
 
 
 def build(ctx_size, queries, keys_in, values_in):
@@ -389,14 +466,15 @@
 
     hbm = pl.BlockSpec(memory_space=pl.ANY)
     dma = pltpu.SemaphoreType.DMA
-    att, cache = pl.pallas_call(
+    parts, stats, cache = pl.pallas_call(
         functools.partial(kernel, heads, kv_heads),
         out_shape=(
-            jax.ShapeDtypeStruct((2 * heads * keep, width), bf16),
+            jax.ShapeDtypeStruct((8, piece, width), bf16),
+            jax.ShapeDtypeStruct((8, 8, piece), f32),
             jax.ShapeDtypeStruct((rows * kv_heads, width), bf16),
         ),
         in_specs=[hbm] * 5,
-        out_specs=(hbm, hbm),
+        out_specs=(hbm, hbm, hbm),
         scratch_shapes=[
             pltpu.VMEM((rows * heads, width), bf16),
             pltpu.VMEM((rows * kv_heads, width), bf16),
@@ -413,19 +491,15 @@
             pltpu.VMEM((8 * piece, 2 * width), f32),
             pltpu.VMEM((NB, CH, RING * 2 * rows), f32),
             pltpu.VMEM((8, piece, width), bf16),
-            pltpu.VMEM((8, piece, width), bf16),
             pltpu.VMEM((8, 8, piece), f32),
-            pltpu.VMEM((8, 8, piece), f32),
-            pltpu.VMEM((2 * heads * keep, width), f32),
-            pltpu.VMEM((2 * heads * keep, width), bf16),
             pltpu.VMEM((rows * kv_heads, width), bf16),
             dma((5,)),
-            dma((2,)),
+            dma((3,)),
             dma,
             dma,
-            dma((RING,)),
-            dma((RING,)),
-            dma((RING - 1, RING)),
+            dma((2 * RING, 2)),
+            dma((RING, 2)),
+            dma((RING, RING)),
             dma((RING, RING)),
             dma((ROW,)),
             dma((ROW,)),
@@ -442,6 +516,17 @@
         jnp.asarray(fine),
         jnp.asarray(coarse),
     )
+    vmem = pl.BlockSpec(memory_space=pltpu.VMEM)
+    att, cache = pl.pallas_call(
+        functools.partial(merge_kernel, heads, group),
+        out_shape=(
+            jax.ShapeDtypeStruct((2 * heads * keep, width), bf16),
+            jax.ShapeDtypeStruct((rows * kv_heads, width), bf16),
+        ),
+        in_specs=[vmem] * 3,
+        out_specs=(vmem, vmem),
+        scratch_shapes=[pltpu.VMEM((2 * heads * keep, width), f32)],
+    )(parts, stats, cache)
     return att.reshape(keep, 2 * heads, width), cache.reshape(rows, kv_heads, width)
 
 

time: 60 us -> 52.4 us (0.87)
  the two profiles are of different devices: /device:TPU:1 before, /device:TPU:449 now
where the time goes in v2:
time: 52.4 us; the launch traced here: 51.7 us
  Pallas kernels  51.1 us (98%)
  between operations  0.64 us (1%)
    pallas_call x1, Pallas kernels, build(): pl.pallas_call(functools.partial(kernel, heads, kv_heads), out_shape=(jax...  49.2 us
    pallas_call x1, Pallas kernels, build(): pl.pallas_call(functools.partial(merge_kernel, heads, group), out_shape=(...  1.89 us

profile of v2, /device:TPU:449, one launch (start us, length us, event | category | flops | bytes accessed | tf_op | source)
XLA Modules:
  0.0 51.7 jit_solution(204513091594455889)
XLA Ops:
  0.6 49.2 %shard_map.68 = (bf16[8,128,128]{2,1,0:T(8,128)(2,1)}, f32[8,8,128]{2,1,0:T(8,128)}, bf16[128,128]{1,0:T(8,128)(2,1)}) custom-call(bf16[512,128]{1,0:T(8,128)(2,1)} %bitcast.5, bf16[128,128]{1,0:T(8,128)(2,1)} %bitcast.6, bf16[128,128]{1,0:T(8,128)(2,1)} %bitcast.7, f32[2,64,128]{2,1,0:T(8,128)} %constant.4.clone.fine_hbm, ...), custom_call_target="tpu_custom_call" | custom-call | tf_op jit(solution)/shard_map/pallas_call | solution.py:469
  49.8 1.9 %shard_map.69 = (bf16[512,128]{1,0:T(8,128)(2,1)}, bf16[128,128]{1,0:T(8,128)(2,1)}) custom-call(bf16[8,128,128]{2,1,0:T(8,128)(2,1)} %get-tuple-element.7.out_recv, f32[8,8,128]{2,1,0:T(8,128)} %get-tuple-element.8.stat_recv, bf16[128,128]{1,0:T(8,128)(2,1)} %get-tuple-element.9.cache_in), custom_call_target="tpu_custom_call" | custom-call | tf_op jit(solution)/shard_map/pallas_call | solution.py:520

commit v3 on v2

--- a/solution.py
+++ b/solution.py
@@ -199,6 +199,8 @@
             device_id_type=MESH,
         )
 
+    spreads = (core == 0) & (u < RING - 1)
+
     def climbs(unit):
         return (core == 1) | ((unit <= u) & (u < RING - 1))
 
@@ -209,7 +211,7 @@
         for i in i_list:
             to = up_by(a, ORDER[i])
 
-            @pl.when((core == 0) | (to > a))
+            @pl.when(spreads | (to > a))
             def _():
                 first_copy(a, half, first_peer(to), i).start()
 
@@ -235,6 +237,14 @@
     for i in range(1, ROW):
         q_copy(own_slot, lax.rem(own_slot + i, ROW), i).start()
     q_all[own_slot] = q_send[core]
+    @pl.when((core == 0) & (u == RING - 1))
+    def _():
+        def clear(f, carry):
+            kv[u, f] = jnp.zeros((2, 2, rows, width), jnp.bfloat16)
+            return carry
+
+        lax.fori_loop(a + 1, RING, clear, 0)
+
     @pl.when(core == 1)
     def _():
         def clear(f, carry):
@@ -263,7 +273,7 @@
     for i in range(1, RING):
         f = up_by(a, ORDER[i])
 
-        @pl.when((core == 0) | (f < a))
+        @pl.when(spreads | (f < a))
         def _():
             for half in range(2):
                 first_copy(f, half, me, i).wait_recv()
@@ -281,7 +291,7 @@
     block_step = along_y * span * 2 + core * (span * 2 * RING)
     row_start = (z_at * RING + y_at) * span * 2
 
-    def absorb(unit):
+    def absorb(unit, order, done):
         key_block = kv[unit, :, :, 0].reshape(keys, width)
         value_block = kv[unit, :, :, 1].reshape(keys, width)
         extended = jnp.concatenate([value_block, jnp.ones_like(value_block)], axis=1)
@@ -289,29 +299,36 @@
         k_at = unit * unit_step + (col // span) * block_step + x_hi * span + col % span - row_start
         at = lax.broadcasted_iota(jnp.int32, (CH, 1), 0)
 
-        def score(r):
-            q = q_all[...].reshape(8 * piece, width)[r * CH : (r + 1) * CH]
+        def score(n):
+            r = order[n]
             scores = factor * lax.dot_general(
-                q, key_block, (((1,), (1,)), ((), ())), preferred_element_type=jnp.float32
+                q_all[r].reshape(CH, width),
+                key_block,
+                (((1,), (1,)), ((), ())),
+                preferred_element_type=jnp.float32,
             )
-            q_at = ((r * CH + at) // piece) * keep + at % keep
-            score_buf[r % NB] = jnp.where(k_at <= q_at, scores, NEVER)
-
-        def weigh(r):
-            take = slice(r * CH, (r + 1) * CH)
+            q_at = (2 * r + at // piece) * keep + at % keep
+            score_buf[n % NB] = jnp.where(k_at <= q_at, scores, NEVER)
+
+        def weigh(n):
+            take = pl.ds(pl.multiple_of(order[n] * CH, CH), CH)
             old = run_max[take, 0:1]
-            top = jnp.maximum(old, jnp.max(score_buf[r % NB], axis=1, keepdims=True))
-            weights = jnp.exp2(score_buf[r % NB] - top).astype(jnp.bfloat16)
+            top = jnp.maximum(old, jnp.max(score_buf[n % NB], axis=1, keepdims=True))
+            weights = jnp.exp2(score_buf[n % NB] - top).astype(jnp.bfloat16)
             total = jnp.dot(weights, extended, preferred_element_type=jnp.float32)
-            run_acc[take, :] = total + jnp.exp2(old - top) * run_acc[take, :]
-            run_max[take, :] = jnp.broadcast_to(top, (CH, width))
-
-        chunks = 8 * piece // CH
+            total = total + jnp.exp2(old - top) * run_acc[take, :]
+            top = jnp.broadcast_to(top, (CH, width))
+            if done is None:
+                run_acc[take, :] = total
+                run_max[take, :] = top
+            else:
+                done(n, total, top)
+
         score(0)
-        for r in range(chunks):
-            if r + 1 < chunks:
-                score(r + 1)
-            weigh(r)
+        for n in range(ROW):
+            if n + 1 < ROW:
+                score(n + 1)
+            weigh(n)
 
     def step_of(step):
         d = (step + 1) // 2
@@ -320,7 +337,7 @@
         far = up_by(u, (2 * odd - 1) * MAJOR)
         return d, odd, unit, far
 
-    def advance(step, carry):
+    def advance(step):
         d, odd, unit, far = step_of(step)
         to = second_peer(far)
 
@@ -347,13 +364,19 @@
                 slot = lax.rem(own_slot + i, ROW)
                 q_copy(slot, own_slot, i).wait_recv()
 
-        @pl.when((unit <= u) | ((core == 1) & (z_at > 0)))
+        return unit, (unit <= u) | ((core == 1) & (z_at > 0))
+
+    def turn_of(step, carry):
+        unit, valid = advance(step)
+
+        @pl.when(valid)
         def _():
-            absorb(unit)
+            absorb(unit, range(ROW), None)
 
         return carry
 
-    lax.fori_loop(0, RING, advance, 0)
+    lax.fori_loop(0, RING - 1, turn_of, 0)
+    last, valid = advance(RING - 1)
 
     def out_copy(slot, d, index):
         return pltpu.make_async_remote_copy(
@@ -375,19 +398,38 @@
             device_id_type=MESH,
         )
 
-    def finish(d):
-        take = pl.ds(pl.multiple_of(d * piece, piece), piece)
-        weight = run_acc[take, width:]
-        stat = run_max[take, :] + math.log2(math.e) * jnp.log(weight)
-        return (run_acc[take, :width] / weight).astype(jnp.bfloat16), stat.T[0:8]
-
-    out_order = (4, 5, 6, 7, 2, 3, 1)
-    for i in out_order:
-        d = lax.rem(place + i, 8)
-        out_send[d], stat_send[d] = finish(d)
-        out_copy(place, d, i).start()
-        stat_copy(place, d, i).start()
-    out_send[place], stat_send[place] = finish(place)
+    across = lax.rem(own_slot + 2, ROW)
+    order = [across, across + 1 - 2 * core, own_slot + 1 - 2 * core, own_slot]
+
+    def finish(n, total, top):
+        for half in range(2):
+            d = order[n] * 2 + half
+            rows_of = slice(half * piece, (half + 1) * piece)
+            weight = total[rows_of, width:]
+            stat = top[rows_of] + math.log2(math.e) * jnp.log(weight)
+            out_send[d] = (total[rows_of, :width] / weight).astype(jnp.bfloat16)
+            stat_send[d] = stat.T[0:8]
+            index = lax.rem(d - place + 8, 8)
+            if n < ROW - 1:
+                out_copy(place, d, index).start()
+                stat_copy(place, d, index).start()
+            else:
+
+                @pl.when(d != place)
+                def _():
+                    out_copy(place, d, index).start()
+                    stat_copy(place, d, index).start()
+
+    @pl.when(valid)
+    def _():
+        absorb(last, order, finish)
+
+    @pl.when(jnp.logical_not(valid))
+    def _():
+        for n in range(ROW):
+            take = pl.ds(pl.multiple_of(order[n] * CH, CH), CH)
+            finish(n, run_acc[take, :], run_max[take, :])
+
     keeps = [
         pltpu.make_async_copy(out_send.at[place], out_recv.at[place], store_sem.at[1]),
         pltpu.make_async_copy(stat_send.at[place], stat_recv.at[place], store_sem.at[2]),
@@ -395,25 +437,17 @@
     for copy in keeps:
         copy.start()
 
-    for i in out_order:
-        slot = lax.rem(place + i, 8)
-        out_copy(slot, place, i).wait_recv()
-        stat_copy(slot, place, i).wait_recv()
-
+    out_order = (4, 5, 6, 7, 2, 3, 1)
     twin_copy(a, u, core).wait_send()
     for i in range(1, RING):
 
-        @pl.when((core == 0) | (up_by(a, ORDER[i]) > a))
+        @pl.when(spreads | (up_by(a, ORDER[i]) > a))
         def _():
             for half in range(2):
                 first_copy(a, half, me, i).wait_send()
 
     for i in range(1, ROW):
         q_copy(own_slot, lax.rem(own_slot + i, ROW), i).wait_send()
-    for i in out_order:
-        out_copy(place, lax.rem(place + i, 8), i).wait_send()
-        stat_copy(place, lax.rem(place + i, 8), i).wait_send()
-
     def drain(slot, carry):
         d = slot // 2
         odd = 1 - slot % 2
@@ -432,6 +466,14 @@
 
     lax.fori_loop(0, RING - 1, drain, 0)
     cache_store.wait()
+    for i in out_order:
+        slot = lax.rem(place + i, 8)
+        out_copy(slot, place, i).wait_recv()
+        stat_copy(slot, place, i).wait_recv()
+
+    for i in out_order:
+        out_copy(place, lax.rem(place + i, 8), i).wait_send()
+        stat_copy(place, lax.rem(place + i, 8), i).wait_send()
     for copy in keeps:
         copy.wait()
 

time: 52.4 us -> 50.7 us (0.968); the launches traced: 51.7 us -> 50.6 us
  Pallas kernels: 51.1 us -> 49.9 us
    pallas_call x1, Pallas kernels: 49.2 us -> 48 us  [build(): pl.pallas_call(functools.partial(kernel, heads, kv_heads), out_shape=(jax...]
where the time goes in v3:
time: 50.7 us; the launch traced here: 50.6 us
  Pallas kernels  49.9 us (98%)
  between operations  0.64 us (1%)
    pallas_call x1, Pallas kernels, build(): pl.pallas_call(functools.partial(kernel, heads, kv_heads), out_shape=(jax...  48 us
    pallas_call x1, Pallas kernels, build(): pl.pallas_call(functools.partial(merge_kernel, heads, group), out_shape=(...  1.89 us

profile of v3, /device:TPU:449, one launch (start us, length us, event | category | flops | bytes accessed | tf_op | source)
XLA Modules:
  0.0 50.6 jit_solution(11545231823696286588)
XLA Ops:
  0.6 48.0 %shard_map.68 = (bf16[8,128,128]{2,1,0:T(8,128)(2,1)}, f32[8,8,128]{2,1,0:T(8,128)}, bf16[128,128]{1,0:T(8,128)(2,1)}) custom-call(bf16[512,128]{1,0:T(8,128)(2,1)} %bitcast.5, bf16[128,128]{1,0:T(8,128)(2,1)} %bitcast.6, bf16[128,128]{1,0:T(8,128)(2,1)} %bitcast.7, f32[2,64,128]{2,1,0:T(8,128)} %constant.4.clone.fine_hbm, ...), custom_call_target="tpu_custom_call" | custom-call | tf_op jit(solution)/shard_map/pallas_call | solution.py:511
  48.7 1.9 %shard_map.69 = (bf16[512,128]{1,0:T(8,128)(2,1)}, bf16[128,128]{1,0:T(8,128)(2,1)}) custom-call(bf16[8,128,128]{2,1,0:T(8,128)(2,1)} %get-tuple-element.7.out_recv, f32[8,8,128]{2,1,0:T(8,128)} %get-tuple-element.8.stat_recv, bf16[128,128]{1,0:T(8,128)(2,1)} %get-tuple-element.9.cache_in), custom_call_target="tpu_custom_call" | custom-call | tf_op jit(solution)/shard_map/pallas_call | solution.py:562

commit v4 on v3

--- a/solution.py
+++ b/solution.py
@@ -199,6 +199,9 @@
             device_id_type=MESH,
         )
 
+    def shares(unit):
+        return ((core == 0) & (unit == 3)) | ((core == 1) & (a == RING - 1))
+
     spreads = (core == 0) & (u < RING - 1)
 
     def climbs(unit):
@@ -325,58 +328,63 @@
                 done(n, total, top)
 
         score(0)
-        for n in range(ROW):
-            if n + 1 < ROW:
+        for n in range(len(order)):
+            if n + 1 < len(order):
                 score(n + 1)
             weigh(n)
 
-    def step_of(step):
-        d = (step + 1) // 2
-        odd = step % 2
-        unit = up_by(u, (1 - 2 * odd) * MAJOR * d)
-        far = up_by(u, (2 * odd - 1) * MAJOR)
-        return d, odd, unit, far
-
-    def advance(step):
-        d, odd, unit, far = step_of(step)
-        to = second_peer(far)
-
-        @pl.when(step > 0)
+    def unit_at(d, odd):
+        return up_by(u, (1 - 2 * odd) * MAJOR * d)
+
+    def counts(unit):
+        return (unit <= u) | ((core == 1) & (z_at > 0))
+
+    def event(d, odd, i):
+        unit = unit_at(d, odd)
+        f = up_by(a, ORDER[i])
+        early = 1 if i < RING // 2 else 0
+        if odd:
+            lands = goes = (core == 1) | (unit < FAR)
+            to = major_to
+        else:
+            lands = (core == 1) | (unit < u)
+            goes = (core == 1) | ((unit < u) & (u < RING - 1))
+            to = minor_to
+        onward = goes & ((d < NEAR) | ((d == NEAR) & (odd == jnp.where(shares(unit), early, 1))))
+
+        @pl.when(lands & ((core == 0) | (f <= a)))
         def _():
-            lands = (core == 1) | jnp.where(odd == 1, unit < FAR, unit < u)
-            goes = (core == 1) | jnp.where(odd == 1, unit < FAR, (unit < u) & (u < RING - 1))
-            goes = goes & (d < NEAR + odd * (FAR - NEAR))
-
-            for i in range(RING):
-                f = up_by(a, ORDER[i])
-
-                @pl.when(lands & ((core == 0) | (f <= a)))
-                def _():
-                    unit_copy(unit, f, me, 0).wait_recv()
-
-                    @pl.when(goes)
-                    def _():
-                        unit_copy(unit, f, to, step + 1).start()
-
-        @pl.when(step == 0)
-        def _():
-            for i in range(1, ROW):
-                slot = lax.rem(own_slot + i, ROW)
-                q_copy(slot, own_slot, i).wait_recv()
-
-        return unit, (unit <= u) | ((core == 1) & (z_at > 0))
-
-    def turn_of(step, carry):
-        unit, valid = advance(step)
-
-        @pl.when(valid)
-        def _():
-            absorb(unit, range(ROW), None)
-
+            unit_copy(unit, f, me, 0).wait_recv()
+
+            @pl.when(onward)
+            def _():
+                unit_copy(unit, f, to, 2 * d + 1 - odd).start()
+
+    def weave(d, d_ready, sides):
+        for g in range(4):
+            for i in range(g * 2, (g + 1) * 2):
+                for odd in sides:
+                    event(d, odd, i)
+            odd = 1 - g // 2
+            unit = unit_at(d_ready, odd)
+            part_of = range(g % 2 * 2, (g % 2 + 1) * 2)
+
+            @pl.when(counts(unit) & ((d_ready > 0) | (odd == 1)))
+            def _():
+                absorb(unit, part_of, None)
+
+    for i in range(1, ROW):
+        slot = lax.rem(own_slot + i, ROW)
+        q_copy(slot, own_slot, i).wait_recv()
+
+    def stage(d, carry):
+        weave(d, d - 1, (1, 0))
         return carry
 
-    lax.fori_loop(0, RING - 1, turn_of, 0)
-    last, valid = advance(RING - 1)
+    lax.fori_loop(1, NEAR + 1, stage, 0)
+    weave(FAR, NEAR, (1,))
+    last = unit_at(FAR, 1)
+    valid = counts(last)
 
     def out_copy(slot, d, index):
         return pltpu.make_async_remote_copy(
@@ -456,15 +464,18 @@
 
         @pl.when(goes)
         def _():
-            for f in range(RING):
-
-                @pl.when((core == 0) | (f <= a))
+            for i in range(RING):
+                f = up_by(a, ORDER[i])
+                early = 1 if i < RING // 2 else 0
+                sent = (d < NEAR) | (odd == jnp.where(shares(unit), early, 1))
+
+                @pl.when(sent & ((core == 0) | (f <= a)))
                 def _():
                     unit_copy(u, f, me, slot).wait_send()
 
         return carry
 
-    lax.fori_loop(0, RING - 1, drain, 0)
+    lax.fori_loop(0, RING, drain, 0)
     cache_store.wait()
     for i in out_order:
         slot = lax.rem(place + i, 8)

time: 50.7 us -> 49.2 us (0.970)
  Pallas kernels: 49.9 us -> 48.4 us
    pallas_call x1, Pallas kernels: 48 us -> 46.5 us  [build(): pl.pallas_call(functools.partial(kernel, heads, kv_heads), out_shape=(jax...]
where the time goes in v4:
time: 49.2 us; the launch traced here: 49.1 us
  Pallas kernels  48.4 us (98%)
  between operations  0.64 us (1%)
    pallas_call x1, Pallas kernels, build(): pl.pallas_call(functools.partial(kernel, heads, kv_heads), out_shape=(jax...  46.5 us
    pallas_call x1, Pallas kernels, build(): pl.pallas_call(functools.partial(merge_kernel, heads, group), out_shape=(...  1.89 us

profile of v4, /device:TPU:449, one launch (start us, length us, event | category | flops | bytes accessed | tf_op | source)
XLA Modules:
  0.0 49.1 jit_solution(4059365053242978464)
XLA Ops:
  0.6 46.5 %shard_map.68 = (bf16[8,128,128]{2,1,0:T(8,128)(2,1)}, f32[8,8,128]{2,1,0:T(8,128)}, bf16[128,128]{1,0:T(8,128)(2,1)}) custom-call(bf16[512,128]{1,0:T(8,128)(2,1)} %bitcast.5, bf16[128,128]{1,0:T(8,128)(2,1)} %bitcast.6, bf16[128,128]{1,0:T(8,128)(2,1)} %bitcast.7, f32[2,64,128]{2,1,0:T(8,128)} %constant.4.clone.fine_hbm, ...), custom_call_target="tpu_custom_call" | custom-call | tf_op jit(solution)/shard_map/pallas_call | solution.py:522
  47.2 1.9 %shard_map.69 = (bf16[512,128]{1,0:T(8,128)(2,1)}, bf16[128,128]{1,0:T(8,128)(2,1)}) custom-call(bf16[8,128,128]{2,1,0:T(8,128)(2,1)} %get-tuple-element.7.out_recv, f32[8,8,128]{2,1,0:T(8,128)} %get-tuple-element.8.stat_recv, bf16[128,128]{1,0:T(8,128)(2,1)} %get-tuple-element.9.cache_in), custom_call_target="tpu_custom_call" | custom-call | tf_op jit(solution)/shard_map/pallas_call | solution.py:573

commit v5 on v4

--- a/solution.py
+++ b/solution.py
@@ -117,6 +117,9 @@
         pltpu.make_async_copy(coarse_hbm.at[me], coarse, load_sem.at[3]),
         pltpu.make_async_copy(q_hbm, q_in, load_sem.at[4]),
     ]
+    for load in loads:
+        load.start()
+
     barrier = pltpu.get_barrier_semaphore()
     for d in range(1, RING):
         to = first_peer(up_by(a, d))
@@ -128,8 +131,6 @@
         to = row_peer(lax.rem(place + i, 8))
         pl.semaphore_signal(barrier, inc=1, device_id=to, device_id_type=MESH)
 
-    for load in loads:
-        load.start()
 
     loads[2].wait()
     loads[3].wait()
@@ -154,9 +155,6 @@
         kv_own[j, 0] = key_rot.astype(jnp.bfloat16)
         kv_own[j, 1] = wide_kv[1, take, :].astype(jnp.bfloat16)
     kv[u, a, core] = kv_own[core]
-    cache_vmem[...] = wide_kv[0].astype(jnp.bfloat16)
-    cache_store = pltpu.make_async_copy(cache_vmem, cache_hbm, store_sem.at[0])
-    cache_store.start()
     pl.semaphore_wait(barrier, (RING - 1) + 2 + 7)
 
     def twin_copy(unit, f, half):
@@ -225,6 +223,9 @@
     twin_copy(a, u, core).start()
     spread(core, (1, 2, 3, 4, 5, 6, 7))
 
+    cache_vmem[...] = wide_kv[0].astype(jnp.bfloat16)
+    cache_store = pltpu.make_async_copy(cache_vmem, cache_hbm, store_sem.at[0])
+    cache_store.start()
     own_slot = me % ROW
     loads[4].wait()
     wide_q[...] = q_in[...].astype(jnp.float32)
@@ -382,7 +383,18 @@
         return carry
 
     lax.fori_loop(1, NEAR + 1, stage, 0)
-    weave(FAR, NEAR, (1,))
+    def settle(n, carry):
+        unit = unit_at(NEAR, 1 - n)
+
+        @pl.when(counts(unit))
+        def _():
+            absorb(unit, range(ROW), None)
+
+        return carry
+
+    lax.fori_loop(0, 2, settle, 0)
+    for i in range(RING):
+        event(FAR, 1, i)
     last = unit_at(FAR, 1)
     valid = counts(last)
 
@@ -561,13 +573,18 @@
             dma((8,)),
             dma((8,)),
         ],
-        compiler_params=pltpu.CompilerParams(collective_id=0, has_side_effects=True),
+        compiler_params=pltpu.CompilerParams(collective_id=0, has_side_effects=True, vmem_limit_bytes=20 * 2**20),
     )(
-        queries.reshape(rows * heads, width),
-        keys_in.reshape(rows * kv_heads, width),
-        values_in.reshape(rows * kv_heads, width),
-        jnp.asarray(fine),
-        jnp.asarray(coarse),
+        *(
+            pltpu.with_memory_space_constraint(x, pltpu.HBM)
+            for x in (
+                queries.reshape(rows * heads, width),
+                keys_in.reshape(rows * kv_heads, width),
+                values_in.reshape(rows * kv_heads, width),
+                jnp.asarray(fine),
+                jnp.asarray(coarse),
+            )
+        )
     )
     vmem = pl.BlockSpec(memory_space=pltpu.VMEM)
     att, cache = pl.pallas_call(
@@ -579,6 +596,7 @@
         in_specs=[vmem] * 3,
         out_specs=(vmem, vmem),
         scratch_shapes=[pltpu.VMEM((2 * heads * keep, width), f32)],
+        compiler_params=pltpu.CompilerParams(vmem_limit_bytes=8 * 2**20),
     )(parts, stats, cache)
     return att.reshape(keep, 2 * heads, width), cache.reshape(rows, kv_heads, width)
 

time: 49.2 us -> 47.1 us (0.957)
  Pallas kernels: 48.4 us -> 46.3 us
    pallas_call x1, Pallas kernels: 46.5 us -> 45.3 us  [build(): pl.pallas_call(functools.partial(kernel, heads, kv_heads), out_shape=(jax...]
    pallas_call x1, Pallas kernels: 1.89 us -> 0.91 us  [build(): pl.pallas_call(functools.partial(merge_kernel, heads, group), out_shape=(...]
where the time goes in v5:
time: 47.1 us; the launch traced here: 46.9 us
  Pallas kernels  46.3 us (98%)
  between operations  0.64 us (1%)
    pallas_call x1, Pallas kernels, build(): pl.pallas_call(functools.partial(kernel, heads, kv_heads), out_shape=(jax...  45.3 us

profile of v5, /device:TPU:449, one launch (start us, length us, event | category | flops | bytes accessed | tf_op | source)
XLA Modules:
  0.0 46.9 jit_solution(9005982530559900280)
XLA Ops:
  0.6 45.3 %shard_map.68 = (bf16[8,128,128]{2,1,0:T(8,128)(2,1)S(1)}, f32[8,8,128]{2,1,0:T(8,128)S(1)}, bf16[128,128]{1,0:T(8,128)(2,1)S(1)}) custom-call(bf16[512,128]{1,0:T(8,128)(2,1)} %bitcast.5, bf16[128,128]{1,0:T(8,128)(2,1)} %bitcast.6, bf16[128,128]{1,0:T(8,128)(2,1)} %bitcast.7, f32[2,64,128]{2,1,0:T(8,128)} %constant.4.clone.fine_hbm, ...), custom_call_target="tpu_custom_call" | custom-call | tf_op jit(solution)/shard_map/pallas_call | solution.py:534
  46.0 0.9 %shard_map.69 = (bf16[512,128]{1,0:T(8,128)(2,1)}, bf16[128,128]{1,0:T(8,128)(2,1)}) custom-call(bf16[8,128,128]{2,1,0:T(8,128)(2,1)S(1)} %get-tuple-element.7.out_recv, f32[8,8,128]{2,1,0:T(8,128)S(1)} %get-tuple-element.8.stat_recv, bf16[128,128]{1,0:T(8,128)(2,1)S(1)} %get-tuple-element.9.cache_in), custom_call_target="tpu_custom_call" | custom-call | tf_op jit(solution)/shard_map/pallas_call | solution.py:590

commit v6 on v5

--- a/solution.py
+++ b/solution.py
@@ -197,9 +197,6 @@
             device_id_type=MESH,
         )
 
-    def shares(unit):
-        return ((core == 0) & (unit == 3)) | ((core == 1) & (a == RING - 1))
-
     spreads = (core == 0) & (u < RING - 1)
 
     def climbs(unit):
@@ -351,7 +348,7 @@
             lands = (core == 1) | (unit < u)
             goes = (core == 1) | ((unit < u) & (u < RING - 1))
             to = minor_to
-        onward = goes & ((d < NEAR) | ((d == NEAR) & (odd == jnp.where(shares(unit), early, 1))))
+        onward = goes & ((d < NEAR) | ((d == NEAR) & (odd == early)))
 
         @pl.when(lands & ((core == 0) | (f <= a)))
         def _():
@@ -363,16 +360,17 @@
 
     def weave(d, d_ready, sides):
         for g in range(4):
+            odd = 1 - g // 2
+            unit = unit_at(d_ready, odd)
+            part_of = range(g % 2 * 2, (g % 2 + 1) * 2)
+
+            @pl.when(counts(unit) & ((d_ready > 0) | (odd == 1)))
+            def _():
+                absorb(unit, part_of, None)
+
             for i in range(g * 2, (g + 1) * 2):
                 for odd in sides:
                     event(d, odd, i)
-            odd = 1 - g // 2
-            unit = unit_at(d_ready, odd)
-            part_of = range(g % 2 * 2, (g % 2 + 1) * 2)
-
-            @pl.when(counts(unit) & ((d_ready > 0) | (odd == 1)))
-            def _():
-                absorb(unit, part_of, None)
 
     for i in range(1, ROW):
         slot = lax.rem(own_slot + i, ROW)
@@ -479,7 +477,7 @@
             for i in range(RING):
                 f = up_by(a, ORDER[i])
                 early = 1 if i < RING // 2 else 0
-                sent = (d < NEAR) | (odd == jnp.where(shares(unit), early, 1))
+                sent = (d < NEAR) | (odd == early)
 
                 @pl.when(sent & ((core == 0) | (f <= a)))
                 def _():

time: 47.1 us -> 46.8 us (level)
  no operation moved by 1% of the time
where the time goes in v6:
time: 46.8 us; the launch traced here: 46.7 us
  Pallas kernels  46 us (98%)
  between operations  0.64 us (1%)
    pallas_call x1, Pallas kernels, build(): pl.pallas_call(functools.partial(kernel, heads, kv_heads), out_shape=(jax...  45.1 us

profile of v6, /device:TPU:449, one launch (start us, length us, event | category | flops | bytes accessed | tf_op | source)
XLA Modules:
  0.0 46.7 jit_solution(5760389016903530007)
XLA Ops:
  0.6 45.1 %shard_map.68 = (bf16[8,128,128]{2,1,0:T(8,128)(2,1)S(1)}, f32[8,8,128]{2,1,0:T(8,128)S(1)}, bf16[128,128]{1,0:T(8,128)(2,1)S(1)}) custom-call(bf16[512,128]{1,0:T(8,128)(2,1)} %bitcast.5, bf16[128,128]{1,0:T(8,128)(2,1)} %bitcast.6, bf16[128,128]{1,0:T(8,128)(2,1)} %bitcast.7, f32[2,64,128]{2,1,0:T(8,128)} %constant.4.clone.fine_hbm, ...), custom_call_target="tpu_custom_call" | custom-call | tf_op jit(solution)/shard_map/pallas_call | solution.py:532
  45.7 0.9 %shard_map.69 = (bf16[512,128]{1,0:T(8,128)(2,1)}, bf16[128,128]{1,0:T(8,128)(2,1)}) custom-call(bf16[8,128,128]{2,1,0:T(8,128)(2,1)S(1)} %get-tuple-element.7.out_recv, f32[8,8,128]{2,1,0:T(8,128)S(1)} %get-tuple-element.8.stat_recv, bf16[128,128]{1,0:T(8,128)(2,1)S(1)} %get-tuple-element.9.cache_in), custom_call_target="tpu_custom_call" | custom-call | tf_op jit(solution)/shard_map/pallas_call | solution.py:588
